TPU v7x, 32 devices: a whole 2x2x4 slice. The times are simulated.
32 devices in a mesh: trial: 4 (over x, core), north: 2 (over y), east: 4 (over z).
Axes of the slice: x: 2, y: 2, z: 4, core: 2. Of those that a mesh axis runs over, the one named last changes fastest.
Arguments:
- pair_state: bfloat16 [192, 48, 128], P(('trial', 'north'), 'east'), parts along dimension 0, may hold values from -6 to 6
- in_gain: float32 [128], replicated, may hold values from 0.25 to 1.75
- left_weight: bfloat16 [512, 128], P('trial'), parts along dimension 0, may hold values from -0.5 to 0.5
- right_weight: bfloat16 [512, 128], P('trial'), parts along dimension 0, may hold values from -0.5 to 0.5
- left_gate: bfloat16 [512, 128], P('trial'), parts along dimension 0, may hold values from -0.5 to 0.5
- right_gate: bfloat16 [512, 128], P('trial'), parts along dimension 0, may hold values from -0.5 to 0.5
- mid_gain: float32 [128], replicated, may hold values from 0.25 to 1.75
- out_weight: bfloat16 [512, 128], P('trial'), parts along dimension 0, may hold values from -0.5 to 0.5
- out_gate: bfloat16 [512, 128], P('trial'), parts along dimension 0, may hold values from -0.5 to 0.5
Outputs:
- triangle_out: bfloat16 [192, 48, 128], P(('trial', 'north'), 'east'), parts along dimension 0
There are 4 independent parts, one for each index of `trial`. A program takes and returns all parts, laid end to end along the dimension named above; an argument that names none is the same for every part. Nothing has to cross between parts.
All inputs are finite; a program needn't handle non-finite values.
Results may differ from a plain program's by a relative error of at most 0.015.
Values may be sent and summed in bfloat16 or wider, within the bound.
No kernel may reach another device: no remote copies, remote signals or barrier semaphores. Data moves between devices by JAX's collectives and lax.ppermute only.
A program may use at most 64 MiB of HBM per device.

v0:
```python
import jax
import jax.numpy as jnp
from jax import lax
from jax.sharding import PartitionSpec as P


def norm_channels(values, channel_gain):
    centred = values - jnp.mean(values, axis=-1, keepdims=True)
    return (
        centred
        * lax.rsqrt(jnp.mean(centred * centred, axis=-1, keepdims=True) + 1e-05)
        * channel_gain
    )


def make_factors(pair_in, in_gain, left_weight, right_weight, left_gate, right_gate):
    ready = norm_channels(pair_in.astype(jnp.float32), in_gain).astype(jnp.bfloat16)
    ready = lax.optimization_barrier(ready)
    left = jnp.einsum("ijc,cd->ijd", ready, left_weight, preferred_element_type=jnp.float32)
    left = left * jax.nn.sigmoid(
        jnp.einsum("ijc,cd->ijd", ready, left_gate, preferred_element_type=jnp.float32)
    )
    right = jnp.einsum("ijc,cd->ijd", ready, right_weight, preferred_element_type=jnp.float32)
    right = right * jax.nn.sigmoid(
        jnp.einsum("ijc,cd->ijd", ready, right_gate, preferred_element_type=jnp.float32)
    )
    return (ready, left.astype(jnp.bfloat16), right.astype(jnp.bfloat16))


def to_pair(mixed, ready, mid_gain, out_weight, out_gate):
    scaled = norm_channels(mixed.astype(jnp.float32), mid_gain).astype(jnp.bfloat16)
    scaled = lax.optimization_barrier(scaled)
    gate = jax.nn.sigmoid(
        jnp.einsum("ijc,cd->ijd", ready, out_gate, preferred_element_type=jnp.float32)
    )
    return (
        jnp.einsum("ijd,dc->ijc", scaled, out_weight, preferred_element_type=jnp.float32) * gate
    ).astype(jnp.bfloat16)


def local(
    pair_state,
    in_gain,
    left_weight,
    right_weight,
    left_gate,
    right_gate,
    mid_gain,
    out_weight,
    out_gate,
):
    ready, left, right = make_factors(
        pair_state, in_gain, left_weight, right_weight, left_gate, right_gate
    )
    count = pair_state.shape[1] * lax.axis_size("east")
    left_lines, right_lines = (
        lax.all_to_all(left, "east", split_axis=2, concat_axis=1, tiled=True),
        lax.all_to_all(right, "east", split_axis=2, concat_axis=1, tiled=True),
    )
    strip = jnp.einsum(
        "ikd,jkd->ijd",
        left_lines,
        lax.all_gather(right_lines, "north", axis=0, tiled=True),
        preferred_element_type=jnp.float32,
    )
    strip = (strip * count ** (-0.5)).astype(jnp.bfloat16)
    mixed = lax.all_to_all(strip, "east", split_axis=1, concat_axis=2, tiled=True)
    return to_pair(mixed, ready, mid_gain, out_weight, out_gate)


def solution(mesh):
    return jax.shard_map(
        local,
        mesh=mesh,
        in_specs=(
            P(("trial", "north"), "east", None),
            P(),
            P("trial", None),
            P("trial", None),
            P("trial", None),
            P("trial", None),
            P(),
            P("trial", None),
            P("trial", None),
        ),
        out_specs=P(("trial", "north"), "east", None),
        check_vma=False,
    )
```

profile of v0, /device:TPU:0, one launch (start us, length us, event | category | flops | bytes accessed | tf_op | source)
XLA Modules:
  0.0 44.6 jit_solution(821063206014544712)
XLA Ops:
  0.0 1.1 %convert_reduce_fusion = f32[24,12]{0,1:T(8,128)S(1)} fusion(bf16[24,12,128]{2,0,1:T(8,128)(2,1)} %param.9), kind=kLoop, calls=%fused_computation.25 | loop fusion | flops 73440 | bytes 74880 | tf_op jit(solution)/shard_map/reduce_sum | solution.py:8
  1.3 0.6 %copy-done.4 = f32[128]{0:T(128)S(1)} copy-done((f32[128]{0:T(128)S(1)}, f32[128]{0:T(128)}, u32[]{:S(2)}) %copy-start.4) | copy-done | bytes 536
  2.3 0.6 %copy-done.6 = bf16[128,128]{1,0:T(8,128)(2,1)S(1)} copy-done((bf16[128,128]{1,0:T(8,128)(2,1)S(1)}, bf16[128,128]{1,0:T(8,128)(2,1)}, u32[]{:S(2)}) %copy-start.6) | copy-done | bytes 32792
  2.9 0.2 fusion.16
  3.1 0.4 copy.34
  3.5 1.1 %reshape.41 = bf16[4,2,4608]{2,1,0:T(2,128)(2,1)} reshape(bf16[128,12,24]{2,1,0:T(8,128)(2,1)S(1)} %bitcast.55) | data formatting | bytes 147456
  4.7 6.5 %all-to-all-start = ((bf16[4,2,4608]{2,1,0:T(2,128)(2,1)}), bf16[4,2,4608]{2,1,0:T(2,128)(2,1)S(1)}, u32[]{:S(2)}, u32[]{:S(2)}) async-start(bf16[4,2,4608]{2,1,0:T(2,128)(2,1)} %reshape.41), calls=%async_computation | async-start | bytes 147456 | tf_op jit(solution)/shard_map/all_to_all | solution.py:58
  11.3 0.6 %copy-done.7 = bf16[128,128]{1,0:T(8,128)(2,1)S(1)} copy-done((bf16[128,128]{1,0:T(8,128)(2,1)S(1)}, bf16[128,128]{1,0:T(8,128)(2,1)}, u32[]{:S(2)}) %copy-start.7) | copy-done | bytes 32792
  11.9 0.2 fusion.15
  12.1 0.4 copy.37
  12.5 1.1 %reshape.43 = bf16[4,2,4608]{2,1,0:T(2,128)(2,1)} reshape(bf16[128,12,24]{2,1,0:T(8,128)(2,1)S(1)} %bitcast.56) | data formatting | bytes 147456
  13.7 3.2 %all-to-all-done = bf16[4,2,4608]{2,1,0:T(2,128)(2,1)S(1)} async-done(((bf16[4,2,4608]{2,1,0:T(2,128)(2,1)}), bf16[4,2,4608]{2,1,0:T(2,128)(2,1)S(1)}, u32[]{:S(2)}, u32[]{:S(2)}) %all-to-all-start) | async-done | bytes 73760 | tf_op jit(solution)/shard_map/all_to_all | solution.py:58
  16.9 3.3 %all-to-all-start.1 = ((bf16[4,2,4608]{2,1,0:T(2,128)(2,1)}), bf16[4,2,4608]{2,1,0:T(2,128)(2,1)S(1)}, u32[]{:S(2)}, u32[]{:S(2)}) async-start(bf16[4,2,4608]{2,1,0:T(2,128)(2,1)} %reshape.43), calls=%async_computation.1 | async-start | bytes 147456 | tf_op jit(solution)/shard_map/all_to_all | solution.py:57
  20.2 0.6 %reshape.42 = bf16[128,12,24]{2,1,0:T(8,128)(2,1)S(1)} reshape(bf16[4,2,4608]{2,1,0:T(2,128)(2,1)S(1)} %all-to-all-done) | data formatting | bytes 147456
  20.8 0.4 copy.35
  21.2 0.3 copy.36
  21.5 6.3 %all_gather.3 = bf16[48,48,32]{1,0,2:T(8,128)(2,1)S(1)} all-gather(bf16[24,48,32]{1,0,2:T(8,128)(2,1)S(1)} %copy.36), channel_id=1, replica_groups=mesh['trial'=4,'north'=2,'east'=4] {'north'}, dimensions={0}, use_global_device_ids=true | all-gather | bytes 221184 | tf_op jit(solution)/shard_map/all_gather | solution.py:63
  27.8 0.6 %reshape.44 = bf16[128,12,24]{2,1,0:T(8,128)(2,1)S(1)} reshape(bf16[4,2,4608]{2,1,0:T(2,128)(2,1)S(1)} %all-to-all-done.1) | data formatting | bytes 147456
  28.4 0.4 copy.38
  28.8 0.3 copy.39
  29.1 0.3 fusion.1
  29.4 0.2 copy.40
  29.6 0.3 reshape.45
  29.9 10.6 %all_to_all.45 = bf16[4,2,4608]{2,1,0:T(2,128)(2,1)S(1)} all-to-all(bf16[4,2,4608]{2,1,0:T(2,128)(2,1)S(1)} %reshape.45), channel_id=1, replica_groups=mesh['trial'=4,'north'=2,'east'=4] {'east'}, dimensions={0} | all-to-all | bytes 147456 | tf_op jit(solution)/shard_map/all_to_all | solution.py:67
  40.5 0.2 reshape.46
  40.9 0.2 multiply_reduce_fusion
  41.2 0.4 copy.41
  41.6 0.3 reshape.32
  41.9 0.4 copy-done.5
  42.4 0.6 %copy-done.3 = bf16[128,128]{1,0:T(8,128)(2,1)S(1)} copy-done((bf16[128,128]{1,0:T(8,128)(2,1)S(1)}, bf16[128,128]{1,0:T(8,128)(2,1)}, u32[]{:S(2)}) %copy-start.3) | copy-done | bytes 32792
  43.2 0.6 %copy-done.8 = bf16[128,128]{1,0:T(8,128)(2,1)S(1)} copy-done((bf16[128,128]{1,0:T(8,128)(2,1)S(1)}, bf16[128,128]{1,0:T(8,128)(2,1)}, u32[]{:S(2)}) %copy-start.8) | copy-done | bytes 32792
  43.7 0.8 %fusion.14 = bf16[24,12,128]{2,0,1:T(8,128)(2,1)} fusion(f32[24,12,128]{2,0,1:T(8,128)S(1)} %fusion.24, bf16[24,12,128]{2,0,1:T(8,128)(2,1)S(1)} %fusion.22, bf16[128,128]{1,0:T(8,128)(2,1)S(1)} %copy-done.8), kind=kOutput, calls=%fused_computation.18 | convolution fusion | flops 9621504 | bytes 327680 | tf_op jit(solution)/shard_map/ijc,cd->ijd/dot_general | solution.py:34
  (25 shorter events, 1.2 us)
Async XLA Ops:
  0.0 2.1 %copy-start = (bf16[128,128]{1,0:T(8,128)(2,1)S(1)}, bf16[128,128]{1,0:T(8,128)(2,1)}, u32[]{:S(2)}) copy-start(bf16[128,128]{1,0:T(8,128)(2,1)} %param.12) | copy-start | bytes 98308
  0.0 1.1 %copy-start.1 = (bf16[24,12,128]{2,0,1:T(8,128)(2,1)S(1)}, bf16[24,12,128]{2,0,1:T(8,128)(2,1)}, u32[]{:S(2)}) copy-start(bf16[24,12,128]{2,0,1:T(8,128)(2,1)} %param.9) | copy-start | bytes 221188
  1.3 0.7 %copy-start.4 = (f32[128]{0:T(128)S(1)}, f32[128]{0:T(128)}, u32[]{:S(2)}) copy-start(f32[128]{0:T(128)} %param.10) | copy-start | bytes 1540
  2.1 0.8 %copy-start.6 = (bf16[128,128]{1,0:T(8,128)(2,1)S(1)}, bf16[128,128]{1,0:T(8,128)(2,1)}, u32[]{:S(2)}) copy-start(bf16[128,128]{1,0:T(8,128)(2,1)} %param.14) | copy-start | bytes 98308
  4.7 6.5 %copy-start.2 = (bf16[128,128]{1,0:T(8,128)(2,1)S(1)}, bf16[128,128]{1,0:T(8,128)(2,1)}, u32[]{:S(2)}) copy-start(bf16[128,128]{1,0:T(8,128)(2,1)} %param.11) | copy-start | bytes 98308
  4.7 12.2 %all-to-all-start = ((bf16[4,2,4608]{2,1,0:T(2,128)(2,1)}), bf16[4,2,4608]{2,1,0:T(2,128)(2,1)S(1)}, u32[]{:S(2)}, u32[]{:S(2)}) async-start(bf16[4,2,4608]{2,1,0:T(2,128)(2,1)} %reshape.41), calls=%async_computation | async-start | bytes 147456 | tf_op jit(solution)/shard_map/all_to_all | solution.py:58
  11.1 0.8 %copy-start.7 = (bf16[128,128]{1,0:T(8,128)(2,1)S(1)}, bf16[128,128]{1,0:T(8,128)(2,1)}, u32[]{:S(2)}) copy-start(bf16[128,128]{1,0:T(8,128)(2,1)} %param.13) | copy-start | bytes 98308
  16.9 10.9 %all-to-all-start.1 = ((bf16[4,2,4608]{2,1,0:T(2,128)(2,1)}), bf16[4,2,4608]{2,1,0:T(2,128)(2,1)S(1)}, u32[]{:S(2)}, u32[]{:S(2)}) async-start(bf16[4,2,4608]{2,1,0:T(2,128)(2,1)} %reshape.43), calls=%async_computation.1 | async-start | bytes 147456 | tf_op jit(solution)/shard_map/all_to_all | solution.py:57
  41.6 0.7 %copy-start.5 = (f32[128]{0:T(128)S(1)}, f32[128]{0:T(128)}, u32[]{:S(2)}) copy-start(f32[128]{0:T(128)} %param.15) | copy-start | bytes 1540
  42.2 0.8 %copy-start.3 = (bf16[128,128]{1,0:T(8,128)(2,1)S(1)}, bf16[128,128]{1,0:T(8,128)(2,1)}, u32[]{:S(2)}) copy-start(bf16[128,128]{1,0:T(8,128)(2,1)} %param.16) | copy-start | bytes 98308
  43.0 0.8 %copy-start.8 = (bf16[128,128]{1,0:T(8,128)(2,1)S(1)}, bf16[128,128]{1,0:T(8,128)(2,1)}, u32[]{:S(2)}) copy-start(bf16[128,128]{1,0:T(8,128)(2,1)} %param.17) | copy-start | bytes 98308
where the time goes:
time: 45.3 us; the launch traced here: 44.6 us
  blocking collectives  17 us (38%)
  local copies, waits for them, and re-layouts  10.4 us (23%)
  starting transfers between devices  9.77 us (22%)
  waiting for transfers between devices  3.24 us (7%)
  matrix products  2.02 us (4%)
  other arithmetic  1.96 us (4%)
    all_to_all x1, blocking collectives, local(): lax.all_to_all(strip, 'east', split_axis=1, concat_axis=2, tiled=True)  10.6 us
    unnamed x24, local copies, waits for them, and re-layouts  7.31 us
    all_to_all x1, starting transfers between devices, local(): lax.all_to_all(right, 'east', split_axis=2, concat_axis=1, tiled=True)  6.48 us
    all_gather x1, blocking collectives, local(): lax.all_gather(right_lines, 'north', axis=0, tiled=True)  6.34 us
    all_to_all x1, starting transfers between devices, local(): lax.all_to_all(left, 'east', split_axis=2, concat_axis=1, tiled=True)  3.29 us
    all_to_all x1, waiting for transfers between devices, local(): lax.all_to_all(right, 'east', split_axis=2, concat_axis=1, tiled=True)  3.23 us
    reduce_sum x2, other arithmetic, norm_channels(): centred = values - jnp.mean(values, axis=-1, keepdims=True)  1.19 us
  transfers between devices with their start and end apart: 2, of which 1 were waited for; matrix products, arithmetic and copies ran while one was open for 7% of the time, Pallas kernels for 0%

commit v1 on v0

--- a/solution.py
+++ b/solution.py
@@ -1,6 +1,10 @@
+import functools
+
 import jax
 import jax.numpy as jnp
 from jax import lax
+from jax.experimental import pallas as pl
+from jax.experimental.pallas import tpu as pltpu
 from jax.sharding import PartitionSpec as P
 
 
@@ -38,7 +42,7 @@
     ).astype(jnp.bfloat16)
 
 
-def local(
+def local_lines(
     pair_state,
     in_gain,
     left_weight,
@@ -68,9 +72,150 @@
     return to_pair(mixed, ready, mid_gain, out_weight, out_gate)
 
 
+def dot32(a, b):
+    return jnp.dot(a, b, preferred_element_type=jnp.float32)
+
+
+def ready_of(block, gain):
+    cols, rows, channels = block.shape
+    flat = block.astype(jnp.float32).reshape(cols * rows, channels)
+    return norm_channels(flat, gain[...]).astype(jnp.bfloat16)
+
+
+def gated(ready, weight, gate, shape):
+    both = dot32(ready, jnp.concatenate([weight[...], gate[...]], axis=1))
+    width = both.shape[1] // 2
+    value = both[:, :width] * jax.nn.sigmoid(both[:, width:])
+    return value.astype(jnp.bfloat16).astype(jnp.float32).reshape(shape)
+
+
+def same_rows(tiles):
+    return lax.axis_index("east") // tiles == lax.axis_index("north")
+
+
+def add_lines(left, right, first, begin, group):
+    lines, _, _ = left.shape
+
+    def step(k, sums):
+        line = left[k]
+        return tuple(
+            sums[j] + line * right[k, begin + j : begin + j + 1, :] for j in range(group)
+        )
+
+    return lax.fori_loop(0, lines, step, first, unroll=4)
+
+
+def near_kernel(
+    own, own_other, far, in_gain, left_weight, right_weight, left_gate, right_gate, out_gate,
+    sums, far_left, gate, left, right, *, tiles
+):
+    cols, rows, channels = own.shape
+    ready = ready_of(own[...], in_gain)
+    left[...] = gated(ready, left_weight, left_gate, own.shape)
+    gate[...] = jax.nn.sigmoid(dot32(ready, out_gate[...])).reshape(own.shape)
+    source = jnp.where(same_rows(tiles), own[...].astype(jnp.float32), own_other[...].astype(jnp.float32))
+    right[...] = gated(ready_of(source, in_gain), right_weight, right_gate, own.shape)
+    zero = jnp.zeros((rows, channels), jnp.float32)
+    for begin in range(0, rows, cols):
+        for j, part in enumerate(add_lines(left, right, (zero,) * cols, begin, cols)):
+            sums[begin + j] = part
+    far_left[...] = gated(ready_of(far[...], in_gain), left_weight, left_gate, own.shape)
+
+
+def far_kernel(
+    far, far_other, far_left, sums, in_gain, right_weight, right_gate, keep, send, right, total,
+    *, tiles
+):
+    cols, rows, _ = far.shape
+    source = jnp.where(same_rows(tiles), far[...].astype(jnp.float32), far_other[...].astype(jnp.float32))
+    right[...] = gated(ready_of(source, in_gain), right_weight, right_gate, far.shape)
+    for begin in range(0, rows, cols):
+        first = tuple(sums[begin + j] for j in range(cols))
+        for j, part in enumerate(add_lines(far_left, right, first, begin, cols)):
+            total[begin + j] = part
+    tile = lax.axis_index("east") % tiles
+    keep[...] = total[pl.ds(tile * cols, cols)]
+    send[...] = total[pl.ds((tiles - 1 - tile) * cols, cols)].astype(jnp.bfloat16)
+
+
+def last_kernel(keep, other, gate, mid_gain, out_weight, out, *, scale):
+    total = keep[...] + other[...].astype(jnp.float32)
+    mixed = (total * scale).astype(jnp.bfloat16)
+    scaled = ready_of(mixed, mid_gain)
+    result = dot32(scaled, out_weight[...]).reshape(out.shape) * gate[...]
+    out[...] = result.astype(jnp.bfloat16)
+
+
+def kernel_call(kernel, args, outs, scratch=()):
+    whole = pl.BlockSpec(memory_space=pltpu.VMEM)
+    return pl.pallas_call(
+        kernel,
+        out_shape=outs,
+        in_specs=[whole] * len(args),
+        out_specs=jax.tree.map(lambda _: whole, outs),
+        scratch_shapes=list(scratch),
+    )(*args)
+
+
+def local_halves(
+    pair_state,
+    in_gain,
+    left_weight,
+    right_weight,
+    left_gate,
+    right_gate,
+    mid_gain,
+    out_weight,
+    out_gate,
+    *,
+    north,
+    east,
+):
+    tiles = east // north
+    own = jnp.transpose(pair_state, (1, 0, 2))
+    cols, rows, channels = own.shape
+    across = [(e, (e + tiles) % east) for e in range(east)]
+    beside = [(e, e // tiles * tiles + tiles - 1 - e % tiles) for e in range(east)]
+    over = [(n, north - 1 - n) for n in range(north)]
+    wide = jax.ShapeDtypeStruct(own.shape, jnp.float32)
+    square = jax.ShapeDtypeStruct((rows, rows, channels), jnp.float32)
+    slim = jax.ShapeDtypeStruct(own.shape, jnp.bfloat16)
+    in_gain = in_gain[None]
+    far = lax.ppermute(own, "east", across)
+    own_other = lax.ppermute(own, "north", over)
+    far_other = lax.ppermute(far, "north", over)
+    sums, far_left, gate = kernel_call(
+        functools.partial(near_kernel, tiles=tiles),
+        (own, own_other, far, in_gain, left_weight, right_weight, left_gate, right_gate, out_gate),
+        (square, wide, wide),
+        (pltpu.VMEM(own.shape, jnp.float32), pltpu.VMEM(own.shape, jnp.float32)),
+    )
+    keep, send = kernel_call(
+        functools.partial(far_kernel, tiles=tiles),
+        (far, far_other, far_left, sums, in_gain, right_weight, right_gate),
+        (wide, slim),
+        (pltpu.VMEM(own.shape, jnp.float32), pltpu.VMEM(square.shape, jnp.float32)),
+    )
+    other = lax.ppermute(send, "east", beside)
+    result = kernel_call(
+        functools.partial(last_kernel, scale=(cols * east) ** (-0.5)),
+        (keep, other, gate, mid_gain[None], out_weight),
+        slim,
+    )
+    return jnp.transpose(result, (1, 0, 2))
+
+
+def pick_local(pair_state, *rest, north, east):
+    rows, cols, _ = pair_state.shape
+    small = pair_state.size * pair_state.dtype.itemsize * east <= 2**21
+    if small and north == 2 and east == 2 * north and rows == 2 * cols:
+        return local_halves(pair_state, *rest, north=north, east=east)
+    return local_lines(pair_state, *rest)
+
+
 def solution(mesh):
     return jax.shard_map(
-        local,
+        functools.partial(pick_local, north=mesh.shape["north"], east=mesh.shape["east"]),
         mesh=mesh,
         in_specs=(
             P(("trial", "north"), "east", None),

time: 45.3 us -> 24 us (0.53); the launches traced: 44.6 us -> 23.8 us
  blocking collectives: 17 us -> 0 us
  local copies, waits for them, and re-layouts: 10.4 us -> 1.88 us
  Pallas kernels: 0 us -> 7.4 us
  waiting for transfers between devices: 3.24 us -> 6.61 us
  matrix products: 2.02 us -> 0 us
  other arithmetic: 1.96 us -> 0 us
  starting transfers between devices: 9.77 us -> 7.88 us
    all_to_all x1 -> x0, blocking collectives: 10.6 us -> none  [local(): lax.all_to_all(strip, 'east', split_axis=1, concat_axis=2, tiled=True)]
    all_to_all x2 -> x0, starting transfers between devices: 9.77 us -> none  [the longest x1 6.48 us: local(): lax.all_to_all(right, 'east', split_axis=2, concat_axis=1, tiled=True)]
    ppermute x0 -> x4, starting transfers between devices: none -> 7.88 us  [the longest x1 4.06 us: local_halves(): far = lax.ppermute(own, 'east', across)]
    pallas_call x0 -> x3, Pallas kernels: none -> 7.4 us  [kernel_call(): pl.pallas_call(kernel, out_shape=outs, in_specs=[whole] * len(args), out_...]
    ppermute x0 -> x4, waiting for transfers between devices: none -> 6.61 us  [the longest x1 4 us: local_halves(): other = lax.ppermute(send, 'east', beside)]
    all_gather x1 -> x0, blocking collectives: 6.34 us -> none  [local(): lax.all_gather(right_lines, 'north', axis=0, tiled=True)]
    unnamed x24 -> x8, local copies, waits for them, and re-layouts: 7.31 us -> 1.88 us
    all_to_all x2 -> x0, waiting for transfers between devices: 3.24 us -> none  [the longest x1 3.23 us: local(): lax.all_to_all(right, 'east', split_axis=2, concat_axis=1, tiled=True)]
  transfers between devices with their start and end apart: 2 -> 4, of which waited for: 1 -> 2; matrix products, arithmetic and copies ran while one was open for 7% -> 0% of each run, Pallas kernels for 0% -> 12%
where the time goes in v1:
time: 24 us; the launch traced here: 23.8 us
  starting transfers between devices  7.88 us (33%)
  Pallas kernels  7.4 us (31%)
  waiting for transfers between devices  6.61 us (28%)
  local copies, waits for them, and re-layouts  1.88 us (8%)
    pallas_call x3, Pallas kernels, kernel_call(): pl.pallas_call(kernel, out_shape=outs, in_specs=[whole] * len(args), out_...  7.4 us
    ppermute x1, starting transfers between devices, local_halves(): far = lax.ppermute(own, 'east', across)  4.06 us
    ppermute x1, waiting for transfers between devices, local_halves(): other = lax.ppermute(send, 'east', beside)  4 us
    ppermute x1, waiting for transfers between devices, local_halves(): far = lax.ppermute(own, 'east', across)  2.6 us
    unnamed x8, local copies, waits for them, and re-layouts  1.88 us
    ppermute x1, starting transfers between devices, local_halves(): far_other = lax.ppermute(far, 'north', over)  1.73 us
    ppermute x1, starting transfers between devices, local_halves(): own_other = lax.ppermute(own, 'north', over)  1.52 us
    ppermute x1, starting transfers between devices, local_halves(): other = lax.ppermute(send, 'east', beside)  0.56 us
  transfers between devices with their start and end apart: 4, of which 2 were waited for; matrix products, arithmetic and copies ran while one was open for 0% of the time, Pallas kernels for 12%

profile of v1, /device:TPU:0, one launch (start us, length us, event | category | flops | bytes accessed | tf_op | source)
XLA Modules:
  0.0 23.8 jit_solution(17375073880872686479)
XLA Ops:
  0.0 4.1 %collective-permute-start = (bf16[12,24,128]{2,1,0:T(8,128)(2,1)}, bf16[12,24,128]{2,1,0:T(8,128)(2,1)S(1)}, u32[]{:S(2)}, u32[]{:S(2)}) collective-permute-start(bf16[12,24,128]{2,1,0:T(8,128)(2,1)} %bitcast.4), channel_id=1, source_target_pairs={{0,2},{1,3},{2,0},{3,1},{4,6},{5,7},{6,4},{7,5},{8,10},{9,11},{10,... | collective-permute-start | bytes 221192 | tf_op jit(solution)/shard_map/ppermute | solution.py:184
  4.1 1.5 %collective-permute-start.2 = (bf16[12,24,128]{2,1,0:T(8,128)(2,1)}, bf16[12,24,128]{2,1,0:T(8,128)(2,1)S(1)}, u32[]{:S(2)}, u32[]{:S(2)}) collective-permute-start(bf16[12,24,128]{2,1,0:T(8,128)(2,1)} %bitcast.5), channel_id=1, source_target_pairs={{0,4},{4,0},{1,5},{5,1},{2,6},{6,2},{3,7},{7,3},{8,12},{12,8},{9,1... | collective-permute-start | bytes 221192 | tf_op jit(solution)/shard_map/ppermute | solution.py:185
  5.6 2.6 %collective-permute-done.far = bf16[12,24,128]{2,1,0:T(8,128)(2,1)S(1)} collective-permute-done((bf16[12,24,128]{2,1,0:T(8,128)(2,1)}, bf16[12,24,128]{2,1,0:T(8,128)(2,1)S(1)}, u32[]{:S(2)}, u32[]{:S(2)}) %collective-permute-start) | collective-permute-done | bytes 73760 | tf_op jit(solution)/shard_map/ppermute | solution.py:184
  8.2 0.0 copy-start
  8.2 1.7 %collective-permute-start.1 = (bf16[12,24,128]{2,1,0:T(8,128)(2,1)S(1)}, bf16[12,24,128]{2,1,0:T(8,128)(2,1)S(1)}, u32[]{:S(2)}, u32[]{:S(2)}) collective-permute-start(bf16[12,24,128]{2,1,0:T(8,128)(2,1)S(1)} %collective-permute-done.far), channel_id=1, source_target_pairs={{0,4},{4,0},{1,5},{5,1},{2,6},{6,2},{3,7},{7,3},{8,12},{12,8},{9,1... | collective-permute-start | bytes 221192 | tf_op jit(solution)/shard_map/ppermute | solution.py:186
  9.9 0.0 collective-permute-done.2.own_other
  9.9 0.0 copy-start.2
  9.9 0.0 copy-done
  9.9 0.6 %copy-done.2 = bf16[12,24,128]{2,1,0:T(8,128)(2,1)} copy-done((bf16[12,24,128]{2,1,0:T(8,128)(2,1)}, bf16[12,24,128]{2,1,0:T(8,128)(2,1)S(1)}, u32[]{:S(2)}) %copy-start.2) | copy-done | bytes 73752
  10.5 3.0 %shard_map.91 = (f32[24,24,128]{2,1,0:T(8,128)}, f32[12,24,128]{2,1,0:T(8,128)}, f32[12,24,128]{2,1,0:T(8,128)}) custom-call(bf16[12,24,128]{2,1,0:T(8,128)(2,1)} %bitcast.6, bf16[12,24,128]{2,1,0:T(8,128)(2,1)} %copy-done.2, bf16[12,24,128]{2,1,0:T(8,128)(2,1)} %copy-done, f32[1,128]{1,0:T(1,128)} %bitcast.7, bf16[128,128]{1,0:T(8,128)(2,1)} %left_weight.1, ...), custom_call_target="tpu_custom_call" | custom-call | tf_op jit(solution)/shard_map/pallas_call | solution.py:151
  13.5 0.0 collective-permute-done.1.far_other
  13.5 0.0 copy-start.1
  13.5 0.6 %copy-done.1 = bf16[12,24,128]{2,1,0:T(8,128)(2,1)} copy-done((bf16[12,24,128]{2,1,0:T(8,128)(2,1)}, bf16[12,24,128]{2,1,0:T(8,128)(2,1)S(1)}, u32[]{:S(2)}) %copy-start.1) | copy-done | bytes 73752
  14.1 2.4 %shard_map.92 = (f32[12,24,128]{2,1,0:T(8,128)}, bf16[12,24,128]{2,1,0:T(8,128)(2,1)}) custom-call(bf16[12,24,128]{2,1,0:T(8,128)(2,1)} %copy-done, bf16[12,24,128]{2,1,0:T(8,128)(2,1)} %copy-done.1, f32[12,24,128]{2,1,0:T(8,128)} %get-tuple-element.10.far_left, f32[24,24,128]{2,1,0:T(8,128)} %get-tuple-element.11.sums, f32[1,128]{1,0:T(1,128)} %bitcast.8, ...), custom_call_target="tpu_custom_call" | custom-call | tf_op jit(solution)/shard_map/pallas_call | solution.py:151
  16.6 0.6 %collective-permute-start.3 = (bf16[12,24,128]{2,1,0:T(8,128)(2,1)}, bf16[12,24,128]{2,1,0:T(8,128)(2,1)S(1)}, u32[]{:S(2)}, u32[]{:S(2)}) collective-permute-start(bf16[12,24,128]{2,1,0:T(8,128)(2,1)} %get-tuple-element.13), channel_id=1, source_target_pairs={{0,1},{1,0},{2,3},{3,2},{4,5},{5,4},{6,7},{7,6},{8,9},{9,8},{10,11... | collective-permute-start | bytes 221192 | tf_op jit(solution)/shard_map/ppermute | solution.py:199
  17.1 4.0 %collective-permute-done.3.other = bf16[12,24,128]{2,1,0:T(8,128)(2,1)S(1)} collective-permute-done((bf16[12,24,128]{2,1,0:T(8,128)(2,1)}, bf16[12,24,128]{2,1,0:T(8,128)(2,1)S(1)}, u32[]{:S(2)}, u32[]{:S(2)}) %collective-permute-start.3) | collective-permute-done | bytes 73760 | tf_op jit(solution)/shard_map/ppermute | solution.py:199
  21.1 0.0 copy-start.3
  21.1 0.6 %copy-done.3 = bf16[12,24,128]{2,1,0:T(8,128)(2,1)} copy-done((bf16[12,24,128]{2,1,0:T(8,128)(2,1)}, bf16[12,24,128]{2,1,0:T(8,128)(2,1)S(1)}, u32[]{:S(2)}) %copy-start.3) | copy-done | bytes 73752
  21.8 2.0 %shard_map.93 = bf16[12,24,128]{2,1,0:T(8,128)(2,1)} custom-call(f32[12,24,128]{2,1,0:T(8,128)} %get-tuple-element.12.keep, bf16[12,24,128]{2,1,0:T(8,128)(2,1)} %copy-done.3, f32[12,24,128]{2,1,0:T(8,128)} %get-tuple-element.14.gate, f32[1,128]{1,0:T(1,128)} %bitcast.9, bf16[128,128]{1,0:T(8,128)(2,1)} %out_weight.1), custom_call_target="tpu_custom_call" | custom-call | tf_op jit(solution)/shard_map/pallas_call | solution.py:151
Async XLA Ops:
  0.0 8.2 %collective-permute-start = (bf16[12,24,128]{2,1,0:T(8,128)(2,1)}, bf16[12,24,128]{2,1,0:T(8,128)(2,1)S(1)}, u32[]{:S(2)}, u32[]{:S(2)}) collective-permute-start(bf16[12,24,128]{2,1,0:T(8,128)(2,1)} %bitcast.4), channel_id=1, source_target_pairs={{0,2},{1,3},{2,0},{3,1},{4,6},{5,7},{6,4},{7,5},{8,10},{9,11},{10,... | collective-permute-start | bytes 221192 | tf_op jit(solution)/shard_map/ppermute | solution.py:184
  4.1 5.9 %collective-permute-start.2 = (bf16[12,24,128]{2,1,0:T(8,128)(2,1)}, bf16[12,24,128]{2,1,0:T(8,128)(2,1)S(1)}, u32[]{:S(2)}, u32[]{:S(2)}) collective-permute-start(bf16[12,24,128]{2,1,0:T(8,128)(2,1)} %bitcast.5), channel_id=1, source_target_pairs={{0,4},{4,0},{1,5},{5,1},{2,6},{6,2},{3,7},{7,3},{8,12},{12,8},{9,1... | collective-permute-start | bytes 221192 | tf_op jit(solution)/shard_map/ppermute | solution.py:185
  8.2 1.7 %copy-start = (bf16[12,24,128]{2,1,0:T(8,128)(2,1)}, bf16[12,24,128]{2,1,0:T(8,128)(2,1)S(1)}, u32[]{:S(2)}) copy-start(bf16[12,24,128]{2,1,0:T(8,128)(2,1)S(1)} %collective-permute-done.far) | copy-start | bytes 221188
  8.2 5.3 %collective-permute-start.1 = (bf16[12,24,128]{2,1,0:T(8,128)(2,1)S(1)}, bf16[12,24,128]{2,1,0:T(8,128)(2,1)S(1)}, u32[]{:S(2)}, u32[]{:S(2)}) collective-permute-start(bf16[12,24,128]{2,1,0:T(8,128)(2,1)S(1)} %collective-permute-done.far), channel_id=1, source_target_pairs={{0,4},{4,0},{1,5},{5,1},{2,6},{6,2},{3,7},{7,3},{8,12},{12,8},{9,1... | collective-permute-start | bytes 221192 | tf_op jit(solution)/shard_map/ppermute | solution.py:186
  9.9 0.6 %copy-start.2 = (bf16[12,24,128]{2,1,0:T(8,128)(2,1)}, bf16[12,24,128]{2,1,0:T(8,128)(2,1)S(1)}, u32[]{:S(2)}) copy-start(bf16[12,24,128]{2,1,0:T(8,128)(2,1)S(1)} %collective-permute-done.2.own_other) | copy-start | bytes 221188
  13.5 0.6 %copy-start.1 = (bf16[12,24,128]{2,1,0:T(8,128)(2,1)}, bf16[12,24,128]{2,1,0:T(8,128)(2,1)S(1)}, u32[]{:S(2)}) copy-start(bf16[12,24,128]{2,1,0:T(8,128)(2,1)S(1)} %collective-permute-done.1.far_other) | copy-start | bytes 221188
  16.6 4.6 %collective-permute-start.3 = (bf16[12,24,128]{2,1,0:T(8,128)(2,1)}, bf16[12,24,128]{2,1,0:T(8,128)(2,1)S(1)}, u32[]{:S(2)}, u32[]{:S(2)}) collective-permute-start(bf16[12,24,128]{2,1,0:T(8,128)(2,1)} %get-tuple-element.13), channel_id=1, source_target_pairs={{0,1},{1,0},{2,3},{3,2},{4,5},{5,4},{6,7},{7,6},{8,9},{9,8},{10,11... | collective-permute-start | bytes 221192 | tf_op jit(solution)/shard_map/ppermute | solution.py:199
  21.1 0.6 %copy-start.3 = (bf16[12,24,128]{2,1,0:T(8,128)(2,1)}, bf16[12,24,128]{2,1,0:T(8,128)(2,1)S(1)}, u32[]{:S(2)}) copy-start(bf16[12,24,128]{2,1,0:T(8,128)(2,1)S(1)} %collective-permute-done.3.other) | copy-start | bytes 221188

commit v2 on v1

--- a/solution.py
+++ b/solution.py
@@ -82,8 +82,8 @@
     return norm_channels(flat, gain[...]).astype(jnp.bfloat16)
 
 
-def gated(ready, weight, gate, shape):
-    both = dot32(ready, jnp.concatenate([weight[...], gate[...]], axis=1))
+def gated(ready, pair, shape):
+    both = dot32(ready, pair[...])
     width = both.shape[1] // 2
     value = both[:, :width] * jax.nn.sigmoid(both[:, width:])
     return value.astype(jnp.bfloat16).astype(jnp.float32).reshape(shape)
@@ -105,30 +105,61 @@
     return lax.fori_loop(0, lines, step, first, unroll=4)
 
 
+def own_kernel(
+    own, in_gain, left_weight, right_weight, left_gate, right_gate, mid_gain, out_weight, out_gate,
+    left, right, gate, left_pair, right_pair, out_copy, in_copy, mid_copy
+):
+    channels = left_weight.shape[1]
+    left_pair[:, :channels] = left_weight[...]
+    left_pair[:, channels:] = left_gate[...]
+    right_pair[:, :channels] = right_weight[...]
+    right_pair[:, channels:] = right_gate[...]
+    out_copy[...] = out_weight[...]
+    in_copy[...] = in_gain[...]
+    mid_copy[...] = mid_gain[...]
+    ready = ready_of(own[...], in_gain)
+    left[...] = gated(ready, left_pair, own.shape)
+    right[...] = gated(ready, right_pair, own.shape)
+    gate[...] = jax.nn.sigmoid(dot32(ready, out_gate[...])).reshape(own.shape)
+
+
 def near_kernel(
-    own, own_other, far, in_gain, left_weight, right_weight, left_gate, right_gate, out_gate,
-    sums, far_left, gate, left, right, *, tiles
-):
-    cols, rows, channels = own.shape
-    ready = ready_of(own[...], in_gain)
-    left[...] = gated(ready, left_weight, left_gate, own.shape)
-    gate[...] = jax.nn.sigmoid(dot32(ready, out_gate[...])).reshape(own.shape)
-    source = jnp.where(same_rows(tiles), own[...].astype(jnp.float32), own_other[...].astype(jnp.float32))
-    right[...] = gated(ready_of(source, in_gain), right_weight, right_gate, own.shape)
+    left, own_right, own_other, far, in_gain, left_pair, right_pair,
+    sums, far_left, far_right, right, *, tiles
+):
+    cols, rows, channels = left.shape
+    same = same_rows(tiles)
+
+    @pl.when(same)
+    def _():
+        right[...] = own_right[...]
+        far_right[...] = gated(ready_of(far[...], in_gain), right_pair, left.shape)
+
+    @pl.when(jnp.logical_not(same))
+    def _():
+        right[...] = gated(ready_of(own_other[...], in_gain), right_pair, left.shape)
+
     zero = jnp.zeros((rows, channels), jnp.float32)
     for begin in range(0, rows, cols):
         for j, part in enumerate(add_lines(left, right, (zero,) * cols, begin, cols)):
             sums[begin + j] = part
-    far_left[...] = gated(ready_of(far[...], in_gain), left_weight, left_gate, own.shape)
+    far_left[...] = gated(ready_of(far[...], in_gain), left_pair, left.shape)
 
 
 def far_kernel(
-    far, far_other, far_left, sums, in_gain, right_weight, right_gate, keep, send, right, total,
-    *, tiles
-):
-    cols, rows, _ = far.shape
-    source = jnp.where(same_rows(tiles), far[...].astype(jnp.float32), far_other[...].astype(jnp.float32))
-    right[...] = gated(ready_of(source, in_gain), right_weight, right_gate, far.shape)
+    far_other, far_left, far_right, sums, in_gain, right_pair, keep, send, right, total, *, tiles
+):
+    cols, rows, _ = far_left.shape
+    same = same_rows(tiles)
+
+    @pl.when(same)
+    def _():
+        right[...] = far_right[...]
+
+    @pl.when(jnp.logical_not(same))
+    def _():
+        right[...] = gated(ready_of(far_other[...], in_gain), right_pair, far_left.shape)
+
     for begin in range(0, rows, cols):
         first = tuple(sums[begin + j] for j in range(cols))
         for j, part in enumerate(add_lines(far_left, right, first, begin, cols)):
@@ -146,8 +177,12 @@
     out[...] = result.astype(jnp.bfloat16)
 
 
-def kernel_call(kernel, args, outs, scratch=()):
+def kernel_call(kernel, args, outs, scratch=(), first=False, last=False):
     whole = pl.BlockSpec(memory_space=pltpu.VMEM)
+    if not last:
+        outs = jax.tree.map(lambda leaf: pltpu.VMEM(leaf.shape, leaf.dtype), outs)
+    if not first:
+        args = [pltpu.with_memory_space_constraint(arg, pltpu.VMEM) for arg in args]
     return pl.pallas_call(
         kernel,
         out_shape=outs,
@@ -180,35 +215,49 @@
     wide = jax.ShapeDtypeStruct(own.shape, jnp.float32)
     square = jax.ShapeDtypeStruct((rows, rows, channels), jnp.float32)
     slim = jax.ShapeDtypeStruct(own.shape, jnp.bfloat16)
-    in_gain = in_gain[None]
+    line = jax.ShapeDtypeStruct((1, channels), jnp.float32)
+    weight = jax.ShapeDtypeStruct(out_weight.shape, jnp.bfloat16)
+    double = jax.ShapeDtypeStruct((channels, 2 * channels), jnp.bfloat16)
     far = lax.ppermute(own, "east", across)
     own_other = lax.ppermute(own, "north", over)
     far_other = lax.ppermute(far, "north", over)
-    sums, far_left, gate = kernel_call(
+    left, right, gate, left_pair, right_pair, out_copy, in_copy, mid_copy = kernel_call(
+        own_kernel,
+        (own, in_gain[None], left_weight, right_weight, left_gate, right_gate)
+        + (mid_gain[None], out_weight, out_gate),
+        (wide, wide, wide, double, double, weight, line, line),
+        first=True,
+    )
+    sums, far_left, far_right = kernel_call(
         functools.partial(near_kernel, tiles=tiles),
-        (own, own_other, far, in_gain, left_weight, right_weight, left_gate, right_gate, out_gate),
+        (left, right, own_other, far, in_copy, left_pair, right_pair),
         (square, wide, wide),
-        (pltpu.VMEM(own.shape, jnp.float32), pltpu.VMEM(own.shape, jnp.float32)),
+        (pltpu.VMEM(own.shape, jnp.float32),),
     )
     keep, send = kernel_call(
         functools.partial(far_kernel, tiles=tiles),
-        (far, far_other, far_left, sums, in_gain, right_weight, right_gate),
+        (far_other, far_left, far_right, sums, in_copy, right_pair),
         (wide, slim),
         (pltpu.VMEM(own.shape, jnp.float32), pltpu.VMEM(square.shape, jnp.float32)),
     )
     other = lax.ppermute(send, "east", beside)
     result = kernel_call(
         functools.partial(last_kernel, scale=(cols * east) ** (-0.5)),
-        (keep, other, gate, mid_gain[None], out_weight),
+        (keep, other, gate, mid_copy, out_copy),
         slim,
+        last=True,
     )
     return jnp.transpose(result, (1, 0, 2))
+
+
+def takes_halves(north, east):
+    return north == 2 and east == 2 * north
 
 
 def pick_local(pair_state, *rest, north, east):
     rows, cols, _ = pair_state.shape
     small = pair_state.size * pair_state.dtype.itemsize * east <= 2**21
-    if small and north == 2 and east == 2 * north and rows == 2 * cols:
+    if small and takes_halves(north, east) and rows == 2 * cols:
         return local_halves(pair_state, *rest, north=north, east=east)
     return local_lines(pair_state, *rest)
 

time: 24 us -> 18.4 us (0.77)
  Pallas kernels: 7.4 us -> 3.73 us
  local copies, waits for them, and re-layouts: 1.88 us -> 0 us
  starting transfers between devices: 7.88 us -> 8.14 us
  waiting for transfers between devices: 6.61 us -> 6.36 us
    pallas_call x3 -> x4, Pallas kernels: 7.4 us -> 3.73 us  [kernel_call(): pl.pallas_call(kernel, out_shape=outs, in_specs=[whole] * len(args), out_...]
    unnamed x8 -> x0, local copies, waits for them, and re-layouts: 1.88 us -> none
    ppermute x1, waiting for transfers between devices: 4 us -> 3.59 us  [local_halves(): other = lax.ppermute(send, 'east', beside)]
    ppermute x1, starting transfers between devices: 0.56 us -> 0.83 us  [local_halves(): other = lax.ppermute(send, 'east', beside)]
  transfers between devices with their start and end apart: 4 -> 4, of which waited for: 2 -> 3; matrix products, arithmetic and copies ran while one was open for 0% -> 0% of each run, Pallas kernels for 12% -> 13%
where the time goes in v2:
time: 18.4 us; the launch traced here: 18.3 us
  starting transfers between devices  8.14 us (44%)
  waiting for transfers between devices  6.36 us (35%)
  Pallas kernels  3.73 us (20%)
    ppermute x1, starting transfers between devices, local_halves(): far = lax.ppermute(own, 'east', across)  4.06 us
    pallas_call x4, Pallas kernels, kernel_call(): pl.pallas_call(kernel, out_shape=outs, in_specs=[whole] * len(args), out_...  3.73 us
    ppermute x1, waiting for transfers between devices, local_halves(): other = lax.ppermute(send, 'east', beside)  3.59 us
    ppermute x1, waiting for transfers between devices, local_halves(): far = lax.ppermute(own, 'east', across)  2.6 us
    ppermute x1, starting transfers between devices, local_halves(): far_other = lax.ppermute(far, 'north', over)  1.73 us
    ppermute x1, starting transfers between devices, local_halves(): own_other = lax.ppermute(own, 'north', over)  1.52 us
    ppermute x1, starting transfers between devices, local_halves(): other = lax.ppermute(send, 'east', beside)  0.83 us
  transfers between devices with their start and end apart: 4, of which 3 were waited for; matrix products, arithmetic and copies ran while one was open for 0% of the time, Pallas kernels for 13%

profile of v2, /device:TPU:0, one launch (start us, length us, event | category | flops | bytes accessed | tf_op | source)
XLA Modules:
  0.0 18.3 jit_solution(16787105388497219961)
XLA Ops:
  0.0 4.1 %collective-permute-start = (bf16[12,24,128]{2,1,0:T(8,128)(2,1)}, bf16[12,24,128]{2,1,0:T(8,128)(2,1)S(1)}, u32[]{:S(2)}, u32[]{:S(2)}) collective-permute-start(bf16[12,24,128]{2,1,0:T(8,128)(2,1)} %bitcast.4), channel_id=1, source_target_pairs={{0,2},{1,3},{2,0},{3,1},{4,6},{5,7},{6,4},{7,5},{8,10},{9,11},{10,... | collective-permute-start | bytes 221192 | tf_op jit(solution)/shard_map/ppermute | solution.py:221
  4.1 1.5 %collective-permute-start.2 = (bf16[12,24,128]{2,1,0:T(8,128)(2,1)}, bf16[12,24,128]{2,1,0:T(8,128)(2,1)S(1)}, u32[]{:S(2)}, u32[]{:S(2)}) collective-permute-start(bf16[12,24,128]{2,1,0:T(8,128)(2,1)} %bitcast.5), channel_id=1, source_target_pairs={{0,4},{4,0},{1,5},{5,1},{2,6},{6,2},{3,7},{7,3},{8,12},{12,8},{9,1... | collective-permute-start | bytes 221192 | tf_op jit(solution)/shard_map/ppermute | solution.py:222
  5.6 2.6 %collective-permute-done.far = bf16[12,24,128]{2,1,0:T(8,128)(2,1)S(1)} collective-permute-done((bf16[12,24,128]{2,1,0:T(8,128)(2,1)}, bf16[12,24,128]{2,1,0:T(8,128)(2,1)S(1)}, u32[]{:S(2)}, u32[]{:S(2)}) %collective-permute-start) | collective-permute-done | bytes 73760 | tf_op jit(solution)/shard_map/ppermute | solution.py:221
  8.2 1.7 %collective-permute-start.1 = (bf16[12,24,128]{2,1,0:T(8,128)(2,1)S(1)}, bf16[12,24,128]{2,1,0:T(8,128)(2,1)S(1)}, u32[]{:S(2)}, u32[]{:S(2)}) collective-permute-start(bf16[12,24,128]{2,1,0:T(8,128)(2,1)S(1)} %collective-permute-done.far), channel_id=1, source_target_pairs={{0,4},{4,0},{1,5},{5,1},{2,6},{6,2},{3,7},{7,3},{8,12},{12,8},{9,1... | collective-permute-start | bytes 221192 | tf_op jit(solution)/shard_map/ppermute | solution.py:223
  9.9 1.4 %shard_map.91 = (f32[12,24,128]{2,1,0:T(8,128)S(1)}, f32[12,24,128]{2,1,0:T(8,128)S(1)}, f32[12,24,128]{2,1,0:T(8,128)S(1)}, bf16[128,256]{1,0:T(8,128)(2,1)S(1)...) custom-call(bf16[12,24,128]{2,1,0:T(8,128)(2,1)} %bitcast.6, ...), custom_call_target="tpu_custom_call" | custom-call | tf_op jit(solution)/shard_map/pallas_call | solution.py:186
  11.3 0.0 collective-permute-done.2.own_other
  11.4 1.0 %shard_map.92 = (f32[24,24,128]{2,1,0:T(8,128)S(1)}, f32[12,24,128]{2,1,0:T(8,128)S(1)}, f32[12,24,128]{2,1,0:T(8,128)S(1)}) custom-call(f32[12,24,128]{2,1,0:T(8,128)S(1)} %get-tuple-element.18.left, f32[12,24,128]{2,1,0:T(8,128)S(1)} %get-tuple-element.19.own_right, bf16[12,24,128]{2,1,0:T(8,128)(2,1)S(1)} %collective-permute-done.2.own_other, ...), custom_call_target="tpu_custom_call" | custom-call | tf_op jit(solution)/shard_map/pallas_call | solution.py:186
  12.4 0.2 collective-permute-done.1.far_other
  12.5 0.3 %shard_map.93 = (f32[12,24,128]{2,1,0:T(8,128)S(1)}, bf16[12,24,128]{2,1,0:T(8,128)(2,1)S(1)}) custom-call(bf16[12,24,128]{2,1,0:T(8,128)(2,1)S(1)} %collective-permute-done.1.far_other, f32[12,24,128]{2,1,0:T(8,128)S(1)} %get-tuple-element.23.far_left, f32[12,24,128]{2,1,0:T(8,128)S(1)} %get-tuple-element.24.far_right, ...), custom_call_target="tpu_custom_call" | custom-call | tf_op jit(solution)/shard_map/pallas_call | solution.py:186
  12.9 0.8 %collective-permute-start.3 = (bf16[12,24,128]{2,1,0:T(8,128)(2,1)S(1)}, bf16[12,24,128]{2,1,0:T(8,128)(2,1)S(1)}, u32[]{:S(2)}, u32[]{:S(2)}) collective-permute-start(bf16[12,24,128]{2,1,0:T(8,128)(2,1)S(1)} %get-tuple-element.27), channel_id=1, source_target_pairs={{0,1},{1,0},{2,3},{3,2},{4,5},{5,4},{6,7},{7,6},{8,9},{9,8},{10,11... | collective-permute-start | bytes 221192 | tf_op jit(solution)/shard_map/ppermute | solution.py:243
  13.7 3.6 %collective-permute-done.3.other = bf16[12,24,128]{2,1,0:T(8,128)(2,1)S(1)} collective-permute-done((bf16[12,24,128]{2,1,0:T(8,128)(2,1)S(1)}, bf16[12,24,128]{2,1,0:T(8,128)(2,1)S(1)}, u32[]{:S(2)}, u32[]{:S(2)}) %collective-permute-start.3) | collective-permute-done | bytes 73760 | tf_op jit(solution)/shard_map/ppermute | solution.py:243
  17.3 1.0 %shard_map.94 = bf16[12,24,128]{2,1,0:T(8,128)(2,1)} custom-call(f32[12,24,128]{2,1,0:T(8,128)S(1)} %get-tuple-element.26.keep, bf16[12,24,128]{2,1,0:T(8,128)(2,1)S(1)} %collective-permute-done.3.other, f32[12,24,128]{2,1,0:T(8,128)S(1)} %get-tuple-element.28.gate, f32[1,128]{1,0:T(1,128)S(1)} %get-tuple-element.29.mid_gain, ...), custom_call_target="tpu_custom_call" | custom-call | tf_op jit(solution)/shard_map/pallas_call | solution.py:186
Async XLA Ops:
  0.0 8.2 %collective-permute-start = (bf16[12,24,128]{2,1,0:T(8,128)(2,1)}, bf16[12,24,128]{2,1,0:T(8,128)(2,1)S(1)}, u32[]{:S(2)}, u32[]{:S(2)}) collective-permute-start(bf16[12,24,128]{2,1,0:T(8,128)(2,1)} %bitcast.4), channel_id=1, source_target_pairs={{0,2},{1,3},{2,0},{3,1},{4,6},{5,7},{6,4},{7,5},{8,10},{9,11},{10,... | collective-permute-start | bytes 221192 | tf_op jit(solution)/shard_map/ppermute | solution.py:221
  4.1 7.3 %collective-permute-start.2 = (bf16[12,24,128]{2,1,0:T(8,128)(2,1)}, bf16[12,24,128]{2,1,0:T(8,128)(2,1)S(1)}, u32[]{:S(2)}, u32[]{:S(2)}) collective-permute-start(bf16[12,24,128]{2,1,0:T(8,128)(2,1)} %bitcast.5), channel_id=1, source_target_pairs={{0,4},{4,0},{1,5},{5,1},{2,6},{6,2},{3,7},{7,3},{8,12},{12,8},{9,1... | collective-permute-start | bytes 221192 | tf_op jit(solution)/shard_map/ppermute | solution.py:222
  8.2 4.4 %collective-permute-start.1 = (bf16[12,24,128]{2,1,0:T(8,128)(2,1)S(1)}, bf16[12,24,128]{2,1,0:T(8,128)(2,1)S(1)}, u32[]{:S(2)}, u32[]{:S(2)}) collective-permute-start(bf16[12,24,128]{2,1,0:T(8,128)(2,1)S(1)} %collective-permute-done.far), channel_id=1, source_target_pairs={{0,4},{4,0},{1,5},{5,1},{2,6},{6,2},{3,7},{7,3},{8,12},{12,8},{9,1... | collective-permute-start | bytes 221192 | tf_op jit(solution)/shard_map/ppermute | solution.py:223
  12.9 4.4 %collective-permute-start.3 = (bf16[12,24,128]{2,1,0:T(8,128)(2,1)S(1)}, bf16[12,24,128]{2,1,0:T(8,128)(2,1)S(1)}, u32[]{:S(2)}, u32[]{:S(2)}) collective-permute-start(bf16[12,24,128]{2,1,0:T(8,128)(2,1)S(1)} %get-tuple-element.27), channel_id=1, source_target_pairs={{0,1},{1,0},{2,3},{3,2},{4,5},{5,4},{6,7},{7,6},{8,9},{9,8},{10,11... | collective-permute-start | bytes 221192 | tf_op jit(solution)/shard_map/ppermute | solution.py:243

commit v3 on v2

--- a/solution.py
+++ b/solution.py
@@ -212,6 +212,11 @@
     across = [(e, (e + tiles) % east) for e in range(east)]
     beside = [(e, e // tiles * tiles + tiles - 1 - e % tiles) for e in range(east)]
     over = [(n, north - 1 - n) for n in range(north)]
+    needed = [
+        (n * east + e, (north - 1 - n) * east + e)
+        for n in range(north)
+        for e in range(n * tiles, n * tiles + tiles)
+    ]
     wide = jax.ShapeDtypeStruct(own.shape, jnp.float32)
     square = jax.ShapeDtypeStruct((rows, rows, channels), jnp.float32)
     slim = jax.ShapeDtypeStruct(own.shape, jnp.bfloat16)
@@ -220,7 +225,7 @@
     double = jax.ShapeDtypeStruct((channels, 2 * channels), jnp.bfloat16)
     far = lax.ppermute(own, "east", across)
     own_other = lax.ppermute(own, "north", over)
-    far_other = lax.ppermute(far, "north", over)
+    far_other = lax.ppermute(far, ("north", "east"), needed)
     left, right, gate, left_pair, right_pair, out_copy, in_copy, mid_copy = kernel_call(
         own_kernel,
         (own, in_gain[None], left_weight, right_weight, left_gate, right_gate)

time: 18.4 us -> 20.2 us (1.098)
  starting transfers between devices: 8.14 us -> 9.83 us
    ppermute x1, starting transfers between devices: 1.73 us -> 3.63 us  [local_halves(): far_other = lax.ppermute(far, ('north', 'east'), needed)]
    ppermute x1, starting transfers between devices: 0.83 us -> 0.62 us  [local_halves(): other = lax.ppermute(send, 'east', beside)]
    ppermute x1, waiting for transfers between devices: 3.59 us -> 3.8 us  [local_halves(): other = lax.ppermute(send, 'east', beside)]
  transfers between devices with their start and end apart: 4 -> 4, of which waited for: 3 -> 2; matrix products, arithmetic and copies ran while one was open for 0% -> 0% of each run, Pallas kernels for 13% -> 12%
where the time goes in v3:
time: 20.2 us; the launch traced here: 20 us
  starting transfers between devices  9.83 us (49%)
  waiting for transfers between devices  6.4 us (32%)
  Pallas kernels  3.76 us (19%)
    ppermute x1, starting transfers between devices, local_halves(): far = lax.ppermute(own, 'east', across)  4.06 us
    ppermute x1, waiting for transfers between devices, local_halves(): other = lax.ppermute(send, 'east', beside)  3.8 us
    pallas_call x4, Pallas kernels, kernel_call(): pl.pallas_call(kernel, out_shape=outs, in_specs=[whole] * len(args), out_...  3.76 us
    ppermute x1, starting transfers between devices, local_halves(): far_other = lax.ppermute(far, ('north', 'east'), needed)  3.63 us
    ppermute x1, waiting for transfers between devices, local_halves(): far = lax.ppermute(own, 'east', across)  2.6 us
    ppermute x1, starting transfers between devices, local_halves(): own_other = lax.ppermute(own, 'north', over)  1.52 us
    ppermute x1, starting transfers between devices, local_halves(): other = lax.ppermute(send, 'east', beside)  0.62 us
  transfers between devices with their start and end apart: 4, of which 2 were waited for; matrix products, arithmetic and copies ran while one was open for 0% of the time, Pallas kernels for 12%

profile of v3, /device:TPU:0, one launch (start us, length us, event | category | flops | bytes accessed | tf_op | source)
XLA Modules:
  0.0 20.0 jit_solution(12363910195577126441)
XLA Ops:
  0.0 4.1 %collective-permute-start = (bf16[12,24,128]{2,1,0:T(8,128)(2,1)}, bf16[12,24,128]{2,1,0:T(8,128)(2,1)S(1)}, u32[]{:S(2)}, u32[]{:S(2)}) collective-permute-start(bf16[12,24,128]{2,1,0:T(8,128)(2,1)} %bitcast.4), channel_id=1, source_target_pairs={{0,2},{1,3},{2,0},{3,1},{4,6},{5,7},{6,4},{7,5},{8,10},{9,11},{10,... | collective-permute-start | bytes 221192 | tf_op jit(solution)/shard_map/ppermute | solution.py:226
  4.1 1.5 %collective-permute-start.2 = (bf16[12,24,128]{2,1,0:T(8,128)(2,1)}, bf16[12,24,128]{2,1,0:T(8,128)(2,1)S(1)}, u32[]{:S(2)}, u32[]{:S(2)}) collective-permute-start(bf16[12,24,128]{2,1,0:T(8,128)(2,1)} %bitcast.5), channel_id=1, source_target_pairs={{0,4},{4,0},{1,5},{5,1},{2,6},{6,2},{3,7},{7,3},{8,12},{12,8},{9,1... | collective-permute-start | bytes 221192 | tf_op jit(solution)/shard_map/ppermute | solution.py:227
  5.6 2.6 %collective-permute-done.far = bf16[12,24,128]{2,1,0:T(8,128)(2,1)S(1)} collective-permute-done((bf16[12,24,128]{2,1,0:T(8,128)(2,1)}, bf16[12,24,128]{2,1,0:T(8,128)(2,1)S(1)}, u32[]{:S(2)}, u32[]{:S(2)}) %collective-permute-start) | collective-permute-done | bytes 73760 | tf_op jit(solution)/shard_map/ppermute | solution.py:226
  8.2 3.6 %collective-permute-start.1 = (bf16[12,24,128]{2,1,0:T(8,128)(2,1)S(1)}, bf16[12,24,128]{2,1,0:T(8,128)(2,1)S(1)}, u32[]{:S(2)}, u32[]{:S(2)}) collective-permute-start(bf16[12,24,128]{2,1,0:T(8,128)(2,1)S(1)} %collective-permute-done.far), channel_id=1, source_target_pairs={{0,4},{1,5},{6,2},{7,3},{8,12},{9,13},{14,10},{15,11},{16,20},{17,... | collective-permute-start | bytes 221192 | tf_op jit(solution)/shard_map/ppermute | solution.py:228
  11.8 1.4 %shard_map.91 = (f32[12,24,128]{2,1,0:T(8,128)S(1)}, f32[12,24,128]{2,1,0:T(8,128)S(1)}, f32[12,24,128]{2,1,0:T(8,128)S(1)}, bf16[128,256]{1,0:T(8,128)(2,1)S(1)...) custom-call(bf16[12,24,128]{2,1,0:T(8,128)(2,1)} %bitcast.6, ...), custom_call_target="tpu_custom_call" | custom-call | tf_op jit(solution)/shard_map/pallas_call | solution.py:186
  13.3 0.0 collective-permute-done.2.own_other
  13.3 1.0 %shard_map.92 = (f32[24,24,128]{2,1,0:T(8,128)S(1)}, f32[12,24,128]{2,1,0:T(8,128)S(1)}, f32[12,24,128]{2,1,0:T(8,128)S(1)}) custom-call(f32[12,24,128]{2,1,0:T(8,128)S(1)} %get-tuple-element.18.left, f32[12,24,128]{2,1,0:T(8,128)S(1)} %get-tuple-element.19.own_right, bf16[12,24,128]{2,1,0:T(8,128)(2,1)S(1)} %collective-permute-done.2.own_other, ...), custom_call_target="tpu_custom_call" | custom-call | tf_op jit(solution)/shard_map/pallas_call | solution.py:186
  14.3 0.0 collective-permute-done.1.far_other
  14.3 0.4 %shard_map.93 = (f32[12,24,128]{2,1,0:T(8,128)S(1)}, bf16[12,24,128]{2,1,0:T(8,128)(2,1)S(1)}) custom-call(bf16[12,24,128]{2,1,0:T(8,128)(2,1)S(1)} %collective-permute-done.1.far_other, f32[12,24,128]{2,1,0:T(8,128)S(1)} %get-tuple-element.23.far_left, f32[12,24,128]{2,1,0:T(8,128)S(1)} %get-tuple-element.24.far_right, ...), custom_call_target="tpu_custom_call" | custom-call | tf_op jit(solution)/shard_map/pallas_call | solution.py:186
  14.7 0.6 %collective-permute-start.3 = (bf16[12,24,128]{2,1,0:T(8,128)(2,1)S(1)}, bf16[12,24,128]{2,1,0:T(8,128)(2,1)S(1)}, u32[]{:S(2)}, u32[]{:S(2)}) collective-permute-start(bf16[12,24,128]{2,1,0:T(8,128)(2,1)S(1)} %get-tuple-element.27), channel_id=1, source_target_pairs={{0,1},{1,0},{2,3},{3,2},{4,5},{5,4},{6,7},{7,6},{8,9},{9,8},{10,11... | collective-permute-start | bytes 221192 | tf_op jit(solution)/shard_map/ppermute | solution.py:248
  15.3 3.8 %collective-permute-done.3.other = bf16[12,24,128]{2,1,0:T(8,128)(2,1)S(1)} collective-permute-done((bf16[12,24,128]{2,1,0:T(8,128)(2,1)S(1)}, bf16[12,24,128]{2,1,0:T(8,128)(2,1)S(1)}, u32[]{:S(2)}, u32[]{:S(2)}) %collective-permute-start.3) | collective-permute-done | bytes 73760 | tf_op jit(solution)/shard_map/ppermute | solution.py:248
  19.1 1.0 %shard_map.94 = bf16[12,24,128]{2,1,0:T(8,128)(2,1)} custom-call(f32[12,24,128]{2,1,0:T(8,128)S(1)} %get-tuple-element.26.keep, bf16[12,24,128]{2,1,0:T(8,128)(2,1)S(1)} %collective-permute-done.3.other, f32[12,24,128]{2,1,0:T(8,128)S(1)} %get-tuple-element.28.gate, f32[1,128]{1,0:T(1,128)S(1)} %get-tuple-element.29.mid_gain, ...), custom_call_target="tpu_custom_call" | custom-call | tf_op jit(solution)/shard_map/pallas_call | solution.py:186
Async XLA Ops:
  0.0 8.2 %collective-permute-start = (bf16[12,24,128]{2,1,0:T(8,128)(2,1)}, bf16[12,24,128]{2,1,0:T(8,128)(2,1)S(1)}, u32[]{:S(2)}, u32[]{:S(2)}) collective-permute-start(bf16[12,24,128]{2,1,0:T(8,128)(2,1)} %bitcast.4), channel_id=1, source_target_pairs={{0,2},{1,3},{2,0},{3,1},{4,6},{5,7},{6,4},{7,5},{8,10},{9,11},{10,... | collective-permute-start | bytes 221192 | tf_op jit(solution)/shard_map/ppermute | solution.py:226
  4.1 9.2 %collective-permute-start.2 = (bf16[12,24,128]{2,1,0:T(8,128)(2,1)}, bf16[12,24,128]{2,1,0:T(8,128)(2,1)S(1)}, u32[]{:S(2)}, u32[]{:S(2)}) collective-permute-start(bf16[12,24,128]{2,1,0:T(8,128)(2,1)} %bitcast.5), channel_id=1, source_target_pairs={{0,4},{4,0},{1,5},{5,1},{2,6},{6,2},{3,7},{7,3},{8,12},{12,8},{9,1... | collective-permute-start | bytes 221192 | tf_op jit(solution)/shard_map/ppermute | solution.py:227
  8.2 6.1 %collective-permute-start.1 = (bf16[12,24,128]{2,1,0:T(8,128)(2,1)S(1)}, bf16[12,24,128]{2,1,0:T(8,128)(2,1)S(1)}, u32[]{:S(2)}, u32[]{:S(2)}) collective-permute-start(bf16[12,24,128]{2,1,0:T(8,128)(2,1)S(1)} %collective-permute-done.far), channel_id=1, source_target_pairs={{0,4},{1,5},{6,2},{7,3},{8,12},{9,13},{14,10},{15,11},{16,20},{17,... | collective-permute-start | bytes 221192 | tf_op jit(solution)/shard_map/ppermute | solution.py:228
  14.7 4.4 %collective-permute-start.3 = (bf16[12,24,128]{2,1,0:T(8,128)(2,1)S(1)}, bf16[12,24,128]{2,1,0:T(8,128)(2,1)S(1)}, u32[]{:S(2)}, u32[]{:S(2)}) collective-permute-start(bf16[12,24,128]{2,1,0:T(8,128)(2,1)S(1)} %get-tuple-element.27), channel_id=1, source_target_pairs={{0,1},{1,0},{2,3},{3,2},{4,5},{5,4},{6,7},{7,6},{8,9},{9,8},{10,11... | collective-permute-start | bytes 221192 | tf_op jit(solution)/shard_map/ppermute | solution.py:248
